TPU v7x, 32 devices: a whole 2x2x4 slice. The times are simulated.
32 devices in a mesh: chan: 4 (over y, x), rows: 8 (over z, core).
Axes of the slice: x: 2, y: 2, z: 4, core: 2. Of those that a mesh axis runs over, the one named last changes fastest.
Arguments:
- residual: float32 [4, 256, 16384], P('chan', 'rows'), may hold values from -6 to 6
- psf: float32 [4, 2048, 2048], P('chan', 'rows'), may hold values from -2 to 2
- positions: int32 [32, 2], replicated, may hold values from 0 to 15360, as said below
Outputs:
- residual_out: float32 [4, 256, 16384], P('chan', 'rows')
- normalized: float32 [256, 16384], P('rows', 'chan')
Inputs may be any that keep to these rules, and one draw needn't show every extreme that they name: positions[k, 0] is a row of the image, 0 to 255; positions[k, 1] is a column from 1024 to 15360.
All inputs are finite; a program needn't handle non-finite values.
Results may differ from a plain program's by a relative error of at most 0.0001.
Values sent between devices are 32-bit elements; how exact they have to be, the bound alone decides.
A program may use at most 128 MiB of HBM per device.

v0:
```python
import jax
import jax.numpy as jnp
from jax import lax
from jax.sharding import PartitionSpec as P

STEPS = 32


def on_device(residual, psf, positions):
    chan_id = lax.axis_index("chan")
    nchan = lax.axis_size("chan")
    row_id = lax.axis_index("rows")
    nrows = lax.axis_size("rows")
    slab = residual.shape[1]
    ncols = residual.shape[2]
    own_psf = psf[0]
    shard_rows = own_psf.shape[0]
    patch = own_psf.shape[1]
    half = patch // 2
    first = row_id * slab
    chan_hot = (jnp.arange(nchan) == chan_id).astype(jnp.float32)
    full_psf = lax.all_gather(own_psf, "rows", axis=0, tiled=True)
    padded_psf = jnp.pad(full_psf, ((slab, slab), (0, 0)))
    zero = jnp.int32(0)

    def subtract(image, row, col, amount):
        offset = first - row + half
        touches = jnp.logical_and(offset > -slab, offset < patch)
        start = jnp.clip(offset + slab, 0, patch + slab)
        psf_rows = lax.dynamic_slice(padded_psf, (start, zero), (slab, patch))
        window = lax.dynamic_slice(image, (zero, col - half), (slab, patch))
        scale = jnp.where(touches, amount, 0.0)
        return lax.dynamic_update_slice(image, window - scale * psf_rows, (zero, col - half))

    image = residual[0]
    peak_rows = positions[:, 0]
    peak_cols = positions[:, 1]
    inside = jnp.logical_and(peak_rows >= first, peak_rows < first + slab)
    local_rows = jnp.clip(peak_rows - first, 0, slab - 1)
    start_values = jnp.where(inside, image[local_rows, peak_cols], 0.0)
    row_offset = peak_rows[:, None] - peak_rows[None, :] + half - row_id * shard_rows
    col_offset = peak_cols[:, None] - peak_cols[None, :] + half
    owned = (row_offset >= 0) & (row_offset < shard_rows) & (col_offset >= 0) & (col_offset < patch)
    couple = own_psf[jnp.clip(row_offset, 0, shard_rows - 1), jnp.clip(col_offset, 0, patch - 1)]
    couple = jnp.where(owned, couple, 0.0)
    start_table, couple_table = lax.psum(
        (chan_hot[:, None] * start_values[None, :], chan_hot[:, None, None] * couple[None, :, :]),
        ("chan", "rows"),
    )

    def solve(k, amps):
        taken = jnp.sum(amps * lax.dynamic_index_in_dim(couple_table, k, 1, False), axis=1)
        value = lax.dynamic_index_in_dim(start_table, k, 1, False) - taken
        amp = 0.25 * (value + jnp.sum(value) / nchan)
        return lax.dynamic_update_index_in_dim(amps, amp, k, 1)

    amps = lax.fori_loop(0, STEPS, solve, jnp.zeros((nchan, STEPS), jnp.float32))
    own_amps = jnp.sum(chan_hot[:, None] * amps, axis=0)

    def apply(k, image):
        return subtract(image, positions[k, 0], positions[k, 1], own_amps[k])

    image = lax.fori_loop(0, STEPS, apply, image)
    count = slab * nrows * ncols
    parts = lax.psum_scatter(image, "chan", scatter_dimension=1, tiled=True)
    total = lax.psum(jnp.sum(parts * parts), ("chan", "rows"))
    normalized = parts * lax.rsqrt(total / count + 1e-06)
    return (image[None], normalized)


def solution(mesh):
    return jax.shard_map(
        on_device,
        mesh=mesh,
        in_specs=(P("chan", "rows", None), P("chan", "rows", None), P()),
        out_specs=(P("chan", "rows", None), P("rows", "chan")),
        check_vma=False,
    )
```

profile of v0, /device:TPU:0, one launch (start us, length us, event | category | flops | bytes accessed | tf_op | source)
XLA Modules:
  0.0 488.9 jit_solution(8474311670628880495)
XLA Ops:
  7.2 3.0 copy.28
  11.9 8.6 %gather_fusion.1 = f32[1024]{0:T(1024)S(1)} fusion(f32[256,2048]{1,0:T(8,128)S(1)} %bitcast.46, s32[1024]{0:T(1024)S(1)} %reshape.252), kind=kCustom, calls=%fused_computation.1 | custom fusion | bytes 16384 | tf_op jit(solution)/shard_map/gather | solution.py:44
  20.5 1.7 gather_fusion
  22.5 50.0 %all-reduce.1 = (f32[4,32]{1,0:T(4,128)S(1)}, f32[4,32,32]{2,0,1:T(4,128)S(1)}) all-reduce(f32[4,32]{1,0:T(4,128)S(1)} %broadcast_multiply_fusion.2, f32[4,32,32]{2,0,1:T(4,128)S(1)} %broadcast_multiply_fusion.1), channel_id=1, replica_groups=mesh['chan'=4,'rows'=8] {'chan','rows'}, use_global_device_ids=true, to_apply=%region_1.2 | all-reduce | flops 4224 | bytes 33792 | tf_op jit(solution)/shard_map/psum | solution.py:46
  72.5 57.8 %while.30 = (s32[]{:T(128)}, f32[4,32]{1,0:T(4,128)S(1)}, f32[4,32]{1,0:T(4,128)S(1)}, f32[4,32,32]{2,0,1:T(4,128)S(1)}, s32[]{:T(128)}, /*index=5*/f32[]{:T(128)}, s32[]{:T(128)}) while((s32[]{:T(128)}, f32[4,32]{1,0:T(4,128)S(1)}, f32[4,32]{1,0:T(4,128)S(1)}, f32[4,32,32]{2,0,1:T(4,128)S(1)}, s32[]{:T(128)}, /*index=5*/f32[]{:T(128)}, ...), condition=%wide.region_5.6_spmd, body=%wide.region_2.5_spmd.sunk | while | flops 274 | bytes 2329 | solution.py:57
  130.4 34.9 %all-gather.3.cloned.1.call-done = f32[1,2048,2048]{2,1,0:T(8,128)} async-done(((f32[1,256,2048]{2,1,0:T(8,128)}), f32[1,2048,2048]{2,1,0:T(8,128)}) %all-gather.3.cloned.1.call-update) | async-done | bytes 16777232 | tf_op jit(solution)/shard_map/all_gather | solution.py:22
  165.3 11.7 %pad.4 = f32[2112,2048]{1,0:T(8,128)} pad(f32[2048,2048]{1,0:T(8,128)} %bitcast.50, f32[]{:T(128)} %constant.206.clone.1), padding=32_32x0_0 | pad | bytes 34078724 | tf_op jit(solution)/shard_map/jit(_pad)/pad | solution.py:23
  177.0 227.6 %while.31 = (s32[]{:T(128)}, f32[32,16384]{1,0:T(8,128)}, s32[32,2]{0,1:T(2,128)S(1)}, s32[]{:T(128)}, f32[32]{0:T(128)S(1)}, /*index=5*/f32[2112,2048]{1,0:T(8,...) while((s32[]{:T(128)}, f32[32,16384]{1,0:T(8,128)}, ...), condition=%wide.region_8.9_spmd, body=%wide.region_7.8_spmd.sunk | while | flops 131087 | bytes 1311065 | solution.py:63
  180.9 1.2 multiply_subtract_fusion.2
  182.1 2.0 dynamic_update_slice.24
  188.0 1.2 multiply_subtract_fusion.2
  189.2 2.0 dynamic_update_slice.24
  195.2 1.2 multiply_subtract_fusion.2
  196.4 2.0 dynamic_update_slice.24
  202.3 1.2 multiply_subtract_fusion.2
  203.5 2.0 dynamic_update_slice.24
  209.4 1.2 multiply_subtract_fusion.2
  210.6 2.0 dynamic_update_slice.24
  216.6 1.2 multiply_subtract_fusion.2
  217.8 2.0 dynamic_update_slice.24
  223.7 1.2 multiply_subtract_fusion.2
  224.9 2.0 dynamic_update_slice.24
  230.8 1.2 multiply_subtract_fusion.2
  232.0 2.0 dynamic_update_slice.24
  237.9 1.2 multiply_subtract_fusion.2
  239.2 2.0 dynamic_update_slice.24
  245.1 1.2 multiply_subtract_fusion.2
  246.3 2.0 dynamic_update_slice.24
  252.2 1.2 multiply_subtract_fusion.2
  253.4 2.0 dynamic_update_slice.24
  259.3 1.2 multiply_subtract_fusion.2
  260.5 2.0 dynamic_update_slice.24
  266.5 1.2 multiply_subtract_fusion.2
  267.7 2.0 dynamic_update_slice.24
  273.6 1.2 multiply_subtract_fusion.2
  274.8 2.0 dynamic_update_slice.24
  280.7 1.2 multiply_subtract_fusion.2
  281.9 2.0 dynamic_update_slice.24
  287.8 1.2 multiply_subtract_fusion.2
  289.1 2.0 dynamic_update_slice.24
  295.0 1.2 multiply_subtract_fusion.2
  296.2 2.0 dynamic_update_slice.24
  302.1 1.2 multiply_subtract_fusion.2
  303.3 2.0 dynamic_update_slice.24
  309.2 1.2 multiply_subtract_fusion.2
  310.4 2.0 dynamic_update_slice.24
  316.3 1.2 multiply_subtract_fusion.2
  317.5 2.0 dynamic_update_slice.24
  324.6 2.0 dynamic_update_slice.24
  331.7 2.0 dynamic_update_slice.24
  338.9 2.0 dynamic_update_slice.24
  346.0 1.7 dynamic_update_slice.24
  352.8 2.0 dynamic_update_slice.24
  359.9 2.0 dynamic_update_slice.24
  367.1 2.0 dynamic_update_slice.24
  374.2 2.0 dynamic_update_slice.24
  381.2 2.0 dynamic_update_slice.24
  388.4 2.0 dynamic_update_slice.24
  395.5 2.0 dynamic_update_slice.24
  402.6 2.0 dynamic_update_slice.24
  404.7 33.5 %reduce-scatter.2.cloned.1.call-done = f32[32,4096]{1,0:T(8,128)} async-done(((f32[32,16384]{1,0:T(8,128)}), f32[32,4096]{1,0:T(8,128)}) %reduce-scatter.2.cloned.1.call-update) | async-done | bytes 524304 | tf_op jit(solution)/shard_map/reduce_scatter | solution.py:65
  438.2 1.8 multiply_reduce_fusion
  440.0 39.5 %psum.23 = f32[]{:T(128)} all-reduce(f32[]{:T(128)} %multiply_reduce_fusion), channel_id=1, replica_groups=mesh['chan'=4,'rows'=8] {'chan','rows'}, use_global_device_ids=true, to_apply=%region_11.12 | all-reduce | flops 1 | bytes 8 | tf_op jit(solution)/shard_map/psum | solution.py:66
  480.2 1.9 broadcast_multiply_fusion
  (287 shorter events, 91.3 us)
Async XLA Ops:
  7.2 158.1 %all-gather.3.cloned.1.call-start = ((), (), s32[]{:S(2)}) async-start(), calls=%async_computation.2 | async-start | bytes 18874368 | tf_op jit(solution)/shard_map/all_gather | solution.py:22
  10.3 0.7 copy-start.1
  10.3 1.6 copy-start
  10.3 427.9 %reduce-scatter.2.cloned.1.call-start = ((), (), s32[]{:S(2)}) async-start(), calls=%async_computation.1 | async-start | bytes 2621440 | tf_op jit(solution)/shard_map/reduce_scatter | solution.py:65
Sparse Core Ops, SparseCore 0:
  10.4 154.8 all-gather.2
  404.8 33.3 reduce-scatter.1
where the time goes:
time: 492 us; the launch traced here: 489 us
  local copies, waits for them, and re-layouts  140 us (28%)
  loops' own time  108 us (22%)
  blocking collectives  89.5 us (18%)
  other arithmetic  68.9 us (14%)
  waiting for transfers between devices  68.4 us (14%)
  between operations  14.8 us (3%)
    another operation x1, loops' own time, on_device(): image = lax.fori_loop(0, STEPS, apply, image)  85.1 us
    dynamic_update_slice x32, local copies, waits for them, and re-layouts, subtract(): lax.dynamic_update_slice(image, window - scale * psf_rows, (zero, col - h...  64.5 us
    psum x1, blocking collectives, on_device(): lax.psum((chan_hot[:, None] * start_values[None, :], chan_hot[:, None, No...  50 us
    dynamic_slice x64, local copies, waits for them, and re-layouts, apply(): return subtract(image, positions[k, 0], positions[k, 1], own_amps[k])  39.7 us
    psum x1, blocking collectives, on_device(): total = lax.psum(jnp.sum(parts * parts), ('chan', 'rows'))  39.5 us
    sub x32, other arithmetic, subtract(): window - scale * psf_rows  38.4 us
    all_gather x1, waiting for transfers between devices, on_device(): full_psf = lax.all_gather(own_psf, 'rows', axis=0, tiled=True)  34.9 us
    reduce_scatter x1, waiting for transfers between devices, on_device(): parts = lax.psum_scatter(image, 'chan', scatter_dimension=1, tiled=True)  33.5 us
  transfers between devices with their start and end apart: 2, of which 2 were waited for; matrix products, arithmetic and copies ran while one was open for 9% of the time, Pallas kernels for 0%

commit v1 on v0

--- a/solution.py
+++ b/solution.py
@@ -4,6 +4,24 @@
 from jax.sharding import PartitionSpec as P
 
 STEPS = 32
+
+
+def ring_gather(shard, axis, dim):
+    ways, here, hop = (lax.axis_size(axis), lax.axis_index(axis), shard.shape[dim])
+    dims = [n * ways if d == dim else n for d, n in enumerate(shard.shape)]
+    full = lax.dynamic_update_slice_in_dim(
+        jnp.zeros(dims, shard.dtype), shard, here * hop, axis=dim
+    )
+    going_up = going_down = shard
+    for far in range(1, ways // 2 + 1):
+        going_up = lax.ppermute(going_up, axis, [(d, (d + 1) % ways) for d in range(ways)])
+        full = lax.dynamic_update_slice_in_dim(full, going_up, (here - far) % ways * hop, axis=dim)
+        if 2 * far < ways:
+            going_down = lax.ppermute(going_down, axis, [(d, (d - 1) % ways) for d in range(ways)])
+            full = lax.dynamic_update_slice_in_dim(
+                full, going_down, (here + far) % ways * hop, axis=dim
+            )
+    return full
 
 
 def on_device(residual, psf, positions):
@@ -19,7 +37,7 @@
     half = patch // 2
     first = row_id * slab
     chan_hot = (jnp.arange(nchan) == chan_id).astype(jnp.float32)
-    full_psf = lax.all_gather(own_psf, "rows", axis=0, tiled=True)
+    full_psf = ring_gather(own_psf, "rows", 0)
     padded_psf = jnp.pad(full_psf, ((slab, slab), (0, 0)))
     zero = jnp.int32(0)
 

time: 492 us -> 548 us (1.11)
  local copies, waits for them, and re-layouts: 140 us -> 168 us
  waiting for transfers between devices: 68.4 us -> 92.1 us
  starting transfers between devices: 0.08 us -> 12 us
  blocking collectives: 89.5 us -> 79.3 us
    ppermute x0 -> x7, waiting for transfers between devices: none -> 58.7 us  [the longest x4 58.2 us: ring_gather(): lax.ppermute(going_up, axis, [(d, (d + 1) % ways) for d in range(ways)])]
    all_gather x1 -> x0, waiting for transfers between devices: 34.9 us -> none  [on_device(): full_psf = lax.all_gather(own_psf, 'rows', axis=0, tiled=True)]
    gather x2, local copies, waits for them, and re-layouts: 8.65 us -> 26.9 us  [on_device(): own_psf[jnp.clip(row_offset, 0, shard_rows - 1), jnp.clip(col_offset, 0,...]
    ppermute x0 -> x7, starting transfers between devices: none -> 11.9 us  [the longest x3 11.3 us: ring_gather(): lax.ppermute(going_down, axis, [(d, (d - 1) % ways) for d in range(ways)])]
    dynamic_update_slice x0 -> x8, local copies, waits for them, and re-layouts: none -> 11.2 us  [the longest x4 5.62 us: ring_gather(): lax.dynamic_update_slice_in_dim(full, going_up, (here - far) % ways * hop...]
    psum x1, blocking collectives: 50 us -> 39.9 us  [on_device(): lax.psum((chan_hot[:, None] * start_values[None, :], chan_hot[:, None, No...]
  transfers between devices with their start and end apart: 2 -> 8, of which waited for: 2 -> 4; matrix products, arithmetic and copies ran while one was open for 9% -> 14% of each run, Pallas kernels for 0% -> 0%
where the time goes in v1:
time: 548 us; the launch traced here: 543 us
  local copies, waits for them, and re-layouts  168 us (31%)
  loops' own time  109 us (20%)
  waiting for transfers between devices  92.1 us (17%)
  blocking collectives  79.3 us (14%)
  other arithmetic  68 us (12%)
  between operations  15 us (3%)
  starting transfers between devices  12 us (2%)
    another operation x1, loops' own time, on_device(): image = lax.fori_loop(0, STEPS, apply, image)  89.5 us
    dynamic_update_slice x32, local copies, waits for them, and re-layouts, subtract(): lax.dynamic_update_slice(image, window - scale * psf_rows, (zero, col - h...  64.5 us
    ppermute x4, waiting for transfers between devices, ring_gather(): lax.ppermute(going_up, axis, [(d, (d + 1) % ways) for d in range(ways)])  58.2 us
    dynamic_slice x64, local copies, waits for them, and re-layouts, apply(): return subtract(image, positions[k, 0], positions[k, 1], own_amps[k])  42.9 us
    psum x1, blocking collectives, on_device(): lax.psum((chan_hot[:, None] * start_values[None, :], chan_hot[:, None, No...  39.9 us
    psum x1, blocking collectives, on_device(): total = lax.psum(jnp.sum(parts * parts), ('chan', 'rows'))  39.5 us
    sub x32, other arithmetic, subtract(): window - scale * psf_rows  38.4 us
    reduce_scatter x1, waiting for transfers between devices, on_device(): parts = lax.psum_scatter(image, 'chan', scatter_dimension=1, tiled=True)  33.4 us
  transfers between devices with their start and end apart: 8, of which 4 were waited for; matrix products, arithmetic and copies ran while one was open for 14% of the time, Pallas kernels for 0%

profile of v1, /device:TPU:0, one launch (start us, length us, event | category | flops | bytes accessed | tf_op | source)
XLA Modules:
  0.0 543.3 jit_solution(2489638532302241455)
XLA Ops:
  7.2 3.0 copy.36
  10.8 4.0 collective-permute-start.1
  14.8 43.9 %collective-permute-done = f32[256,2048]{1,0:T(8,128)} collective-permute-done((f32[256,2048]{1,0:T(8,128)}, f32[256,2048]{1,0:T(8,128)}, u32[]{:S(2)}, u32[]{:S(2)}) %collective-permute-start) | collective-permute-done | bytes 2097184 | tf_op jit(solution)/shard_map/ppermute | solution.py:17
  59.1 3.8 collective-permute-start.3
  63.8 26.9 %gather_fusion.1 = f32[1024]{0:T(1024)S(1)} fusion(f32[256,2048]{1,0:T(8,128)} %bitcast.48, s32[1024]{0:T(1024)S(1)} %reshape.252), kind=kCustom, calls=%fused_computation.1 | custom fusion | bytes 16384 | tf_op jit(solution)/shard_map/gather | solution.py:62
  90.8 1.6 gather_fusion
  92.7 39.9 %all-reduce.1 = (f32[4,32]{1,0:T(4,128)S(1)}, f32[4,32,32]{2,0,1:T(4,128)S(1)}) all-reduce(f32[4,32]{1,0:T(4,128)S(1)} %broadcast_multiply_fusion.2, f32[4,32,32]{2,0,1:T(4,128)S(1)} %broadcast_multiply_fusion.1), channel_id=1, replica_groups=mesh['chan'=4,'rows'=8] {'chan','rows'}, use_global_device_ids=true, to_apply=%region_1.2 | all-reduce | flops 4224 | bytes 33792 | tf_op jit(solution)/shard_map/psum | solution.py:64
  132.6 3.5 collective-permute-start.5
  136.1 53.4 %while.30 = (s32[]{:T(128)}, f32[4,32]{1,0:T(4,128)S(1)}, f32[4,32]{1,0:T(4,128)S(1)}, f32[4,32,32]{2,0,1:T(4,128)S(1)}, s32[]{:T(128)}, /*index=5*/f32[]{:T(128)}, s32[]{:T(128)}) while((s32[]{:T(128)}, f32[4,32]{1,0:T(4,128)S(1)}, f32[4,32]{1,0:T(4,128)S(1)}, f32[4,32,32]{2,0,1:T(4,128)S(1)}, s32[]{:T(128)}, /*index=5*/f32[]{:T(128)}, ...), condition=%wide.region_5.6_spmd, body=%wide.region_2.5_spmd.sunk | while | flops 274 | bytes 2321 | solution.py:75
  189.8 2.1 broadcast_in_dim.33
  192.1 1.8 constant_dynamic-update-slice_fusion.6
  193.9 1.8 constant_dynamic-update-slice_fusion.5
  195.7 1.8 constant_dynamic-update-slice_fusion.4
  197.5 1.8 constant_dynamic-update-slice_fusion.3
  199.3 1.8 constant_dynamic-update-slice_fusion.2
  201.1 1.8 constant_dynamic-update-slice_fusion.1
  202.9 14.3 %collective-permute-done.6 = f32[256,2048]{1,0:T(8,128)S(1)} collective-permute-done((f32[256,2048]{1,0:T(8,128)}, f32[256,2048]{1,0:T(8,128)S(1)}, u32[]{:S(2)}, u32[]{:S(2)}) %collective-permute-start.6) | collective-permute-done | bytes 2097184 | tf_op jit(solution)/shard_map/ppermute | solution.py:17
  217.5 6.4 %pad.4 = f32[2112,2048]{1,0:T(8,128)} pad(f32[2048,2048]{1,0:T(8,128)S(1)} %constant_dynamic-update-slice_fusion, f32[]{:T(128)} %constant.250.clone.1), padding=32_32x0_0 | pad | bytes 34078724 | tf_op jit(solution)/shard_map/jit(_pad)/pad | solution.py:41
  223.9 235.3 %while.31 = (s32[]{:T(128)}, f32[32,16384]{1,0:T(8,128)}, s32[32,2]{0,1:T(2,128)S(1)}, s32[]{:T(128)}, f32[32]{0:T(128)S(1)}, /*index=5*/f32[2112,2048]{1,0:T(8,...) while((s32[]{:T(128)}, f32[32,16384]{1,0:T(8,128)}, ...), condition=%wide.region_8.9_spmd, body=%wide.region_7.8_spmd.sunk | while | flops 131087 | bytes 1311057 | solution.py:81
  228.1 1.2 multiply_subtract_fusion.2
  229.3 2.0 dynamic_update_slice.64
  235.4 1.2 multiply_subtract_fusion.2
  236.6 2.0 dynamic_update_slice.64
  242.8 1.2 multiply_subtract_fusion.2
  244.0 2.0 dynamic_update_slice.64
  250.2 1.2 multiply_subtract_fusion.2
  251.4 2.0 dynamic_update_slice.64
  257.5 1.2 multiply_subtract_fusion.2
  258.7 2.0 dynamic_update_slice.64
  264.9 1.2 multiply_subtract_fusion.2
  266.1 2.0 dynamic_update_slice.64
  272.3 1.2 multiply_subtract_fusion.2
  273.5 2.0 dynamic_update_slice.64
  279.6 1.2 multiply_subtract_fusion.2
  280.9 2.0 dynamic_update_slice.64
  287.0 1.2 multiply_subtract_fusion.2
  288.2 2.0 dynamic_update_slice.64
  295.6 2.0 dynamic_update_slice.64
  303.0 2.0 dynamic_update_slice.64
  310.3 2.0 dynamic_update_slice.64
  317.7 2.0 dynamic_update_slice.64
  325.1 2.0 dynamic_update_slice.64
  332.4 2.0 dynamic_update_slice.64
  339.8 2.0 dynamic_update_slice.64
  347.2 2.0 dynamic_update_slice.64
  354.5 2.0 dynamic_update_slice.64
  361.9 2.0 dynamic_update_slice.64
  369.2 2.0 dynamic_update_slice.64
  376.6 2.0 dynamic_update_slice.64
  383.9 2.0 dynamic_update_slice.64
  391.3 2.0 dynamic_update_slice.64
  398.7 1.7 dynamic_update_slice.64
  405.7 2.0 dynamic_update_slice.64
  413.1 2.0 dynamic_update_slice.64
  420.4 2.0 dynamic_update_slice.64
  427.8 2.0 dynamic_update_slice.64
  435.1 2.0 dynamic_update_slice.64
  442.5 2.0 dynamic_update_slice.64
  449.8 2.0 dynamic_update_slice.64
  457.2 2.0 dynamic_update_slice.64
  459.3 33.4 %reduce-scatter.2.cloned.1.call-done = f32[32,4096]{1,0:T(8,128)} async-done(((f32[32,16384]{1,0:T(8,128)}), f32[32,4096]{1,0:T(8,128)}) %reduce-scatter.2.cloned.1.call-update) | async-done | bytes 524304 | tf_op jit(solution)/shard_map/reduce_scatter | solution.py:83
  492.6 1.8 multiply_reduce_fusion
  494.4 39.5 %psum.23 = f32[]{:T(128)} all-reduce(f32[]{:T(128)} %multiply_reduce_fusion), channel_id=1, replica_groups=mesh['chan'=4,'rows'=8] {'chan','rows'}, use_global_device_ids=true, to_apply=%region_11.12 | all-reduce | flops 1 | bytes 8 | tf_op jit(solution)/shard_map/psum | solution.py:84
  534.6 1.9 broadcast_multiply_fusion
  (307 shorter events, 107.0 us)
Async XLA Ops:
  7.2 85.2 %copy-start.1 = (s32[32,2]{0,1:T(2,128)S(1)}, s32[32,2]{0,1:T(2,128)}, u32[]{:S(2)}) copy-start(s32[32,2]{0,1:T(2,128)} %param.9) | copy-start | bytes 772
  7.2 485.5 %reduce-scatter.2.cloned.1.call-start = ((), (), s32[]{:S(2)}) async-start(), calls=%async_computation.1 | async-start | bytes 2621440 | tf_op jit(solution)/shard_map/reduce_scatter | solution.py:83
  10.3 48.4 %collective-permute-start = (f32[256,2048]{1,0:T(8,128)}, f32[256,2048]{1,0:T(8,128)}, u32[]{:S(2)}, u32[]{:S(2)}) collective-permute-start(f32[256,2048]{1,0:T(8,128)} %bitcast.46), channel_id=1, source_target_pairs={{0,1},{1,2},{2,3},{3,4},{4,5},{5,6},{6,7},{7,0},{8,9},{9,10},{10,1... | collective-permute-start | bytes 6291464 | tf_op jit(solution)/shard_map/ppermute | solution.py:17
  10.8 48.4 %collective-permute-start.1 = (f32[256,2048]{1,0:T(8,128)}, f32[256,2048]{1,0:T(8,128)}, u32[]{:S(2)}, u32[]{:S(2)}) collective-permute-start(f32[256,2048]{1,0:T(8,128)} %bitcast.47), channel_id=1, source_target_pairs={{0,7},{1,0},{2,1},{3,2},{4,3},{5,4},{6,5},{7,6},{8,15},{9,8},{10,9... | collective-permute-start | bytes 6291464 | tf_op jit(solution)/shard_map/ppermute | solution.py:20
  58.7 73.8 %collective-permute-start.2 = (f32[256,2048]{1,0:T(8,128)}, f32[256,2048]{1,0:T(8,128)}, u32[]{:S(2)}, u32[]{:S(2)}) collective-permute-start(f32[256,2048]{1,0:T(8,128)} %collective-permute-done), channel_id=1, source_target_pairs={{0,1},{1,2},{2,3},{3,4},{4,5},{5,6},{6,7},{7,0},{8,9},{9,10},{10,1... | collective-permute-start | bytes 6291464 | tf_op jit(solution)/shard_map/ppermute | solution.py:17
  59.1 73.5 %collective-permute-start.3 = (f32[256,2048]{1,0:T(8,128)}, f32[256,2048]{1,0:T(8,128)}, u32[]{:S(2)}, u32[]{:S(2)}) collective-permute-start(f32[256,2048]{1,0:T(8,128)} %collective-permute-done.1), channel_id=1, source_target_pairs={{0,7},{1,0},{2,1},{3,2},{4,3},{5,4},{6,5},{7,6},{8,15},{9,8},{10,9... | collective-permute-start | bytes 6291464 | tf_op jit(solution)/shard_map/ppermute | solution.py:20
  63.8 128.1 %copy-start = (f32[1,256,2048]{2,1,0:T(8,128)S(1)}, f32[1,256,2048]{2,1,0:T(8,128)}, u32[]{:S(2)}) copy-start(f32[1,256,2048]{2,1,0:T(8,128)} %param.8) | copy-start | bytes 6291460
  132.5 57.2 %collective-permute-start.4 = (f32[256,2048]{1,0:T(8,128)}, f32[256,2048]{1,0:T(8,128)}, u32[]{:S(2)}, u32[]{:S(2)}) collective-permute-start(f32[256,2048]{1,0:T(8,128)} %collective-permute-done.2), channel_id=1, source_target_pairs={{0,1},{1,2},{2,3},{3,4},{4,5},{5,6},{6,7},{7,0},{8,9},{9,10},{10,1... | collective-permute-start | bytes 6291464 | tf_op jit(solution)/shard_map/ppermute | solution.py:17
  132.6 68.5 %collective-permute-start.5 = (f32[256,2048]{1,0:T(8,128)}, f32[256,2048]{1,0:T(8,128)}, u32[]{:S(2)}, u32[]{:S(2)}) collective-permute-start(f32[256,2048]{1,0:T(8,128)} %collective-permute-done.3), channel_id=1, source_target_pairs={{0,7},{1,0},{2,1},{3,2},{4,3},{5,4},{6,5},{7,6},{8,15},{9,8},{10,9... | collective-permute-start | bytes 6291464 | tf_op jit(solution)/shard_map/ppermute | solution.py:20
  189.7 27.5 %collective-permute-start.6 = (f32[256,2048]{1,0:T(8,128)}, f32[256,2048]{1,0:T(8,128)S(1)}, u32[]{:S(2)}, u32[]{:S(2)}) collective-permute-start(f32[256,2048]{1,0:T(8,128)} %collective-permute-done.4), channel_id=1, source_target_pairs={{0,1},{1,2},{2,3},{3,4},{4,5},{5,6},{6,7},{7,0},{8,9},{9,10},{10,1... | collective-permute-start | bytes 6291464 | tf_op jit(solution)/shard_map/ppermute | solution.py:17
Sparse Core Ops, SparseCore 0:
  459.4 33.2 reduce-scatter.1
